TPU v7x, 32 devices: a whole 2x2x4 slice. The times are simulated.
32 devices in a mesh: dp: 16 (over z, x, core), stream: 2 (over y).
Axes of the slice: x: 2, y: 2, z: 4, core: 2. Of those that a mesh axis runs over, the one named last changes fastest.
Arguments:
- tokens: bfloat16 [80, 2, 200, 768], P('dp', 'stream'), may hold values from -6 to 6
- text_segment: int32 [80, 200], P('dp'), may hold values from 0 to 5, as said below
- ln1_gain: float32 [768], replicated, may hold values from 0.5 to 1.5
- ln1_bias: float32 [768], replicated, may hold values from -3 to 3
- qkv_weight: bfloat16 [768, 2304], replicated, may hold values from -0.3125 to 0.3125
- out_weight: bfloat16 [768, 768], replicated, may hold values from -0.625 to 0.625
- attn_scale: float32 [768], replicated, may hold values from 0.25 to 1.75
- ffn_scale: float32 [768], replicated, may hold values from 0.25 to 1.75
- ln2_gain: float32 [2, 768], P('stream'), may hold values from 0.5 to 1.5
- ln2_bias: float32 [2, 768], P('stream'), may hold values from -3 to 3
- expert_in: bfloat16 [2, 768, 3072], P('stream'), may hold values from -0.21875 to 0.21875
- expert_out: bfloat16 [2, 3072, 768], P('stream'), may hold values from -0.15625 to 0.15625
- out_cot: bfloat16 [80, 2, 200, 768], P('dp', 'stream'), may hold values from -6 to 6
Outputs:
- block_out: bfloat16 [80, 2, 200, 768], P('dp', 'stream')
- tokens_grad: bfloat16 [80, 2, 200, 768], P('dp', 'stream')
- ln1_gain_grad: float32 [768], replicated
- ln1_bias_grad: float32 [768], replicated
- qkv_weight_grad: float32 [768, 2304], replicated
- out_weight_grad: float32 [768, 768], replicated
- attn_scale_grad: float32 [768], replicated
- ffn_scale_grad: float32 [768], replicated
- ln2_gain_grad: float32 [2, 768], P('stream')
- ln2_bias_grad: float32 [2, 768], P('stream')
- expert_in_grad: float32 [2, 768, 3072], P('stream')
- expert_out_grad: float32 [2, 3072, 768], P('stream')
Inputs may be any that keep to these rules, and one draw needn't show every extreme that they name: `text_segment`: in each group the text slots hold the captions numbered below 5 in order, each of 1 to 39 slots, followed by padding slots numbered 5.
All inputs are finite; a program needn't handle non-finite values.
Results may differ from a plain program's by a relative error of at most 0.015.
The roundings to bfloat16 on the way count: a program that leaves them out, or rounds other values in their place, can miss the bound.
Values may be sent and summed in bfloat16 or wider, within the bound.
A program may use at most 256 MiB of HBM per device.

v0:
```python
import jax
import jax.numpy as jnp
from jax import lax
from jax.sharding import PartitionSpec as P

HEADS = 12
HDIM = 64
PATCHES = 197
CAPTIONS = 5
EPSILON = 1e-05


def layer_norm(inputs, gain_row, bias_row):
    row_mean = jnp.mean(inputs, axis=-1, keepdims=True)
    centered = inputs - row_mean
    variance = jnp.mean(centered * centered, axis=-1, keepdims=True)
    return centered * lax.rsqrt(variance + EPSILON) * gain_row + bias_row


def gelu_exact(inputs):
    return jax.nn.gelu(inputs, approximate=False)


def contract_rows(left_side, right_side):
    return lax.dot_general(
        left_side, right_side, (((0,), (0,)), ((), ())), preferred_element_type=jnp.float32
    )


def times_transposed(left_side, right_side):
    return lax.dot_general(
        left_side, right_side, (((1,), (1,)), ((), ())), preferred_element_type=jnp.float32
    )


def shards(
    tokens,
    text_segment,
    ln1_gain,
    ln1_bias,
    qkv_weight,
    out_weight,
    attn_scale,
    ffn_scale,
    ln2_gain,
    ln2_bias,
    expert_in,
    expert_out,
    out_cot,
):
    group_count = tokens.shape[0]
    slot_count = tokens.shape[2]
    model_width = tokens.shape[3]
    row_count = group_count * slot_count
    score_scale = HDIM ** (-0.5)
    stream_index = lax.axis_index("stream")
    flat_rows = tokens.reshape(row_count, model_width).astype(jnp.float32)
    attn_in, ln1_pull = jax.vjp(layer_norm, flat_rows, ln1_gain, ln1_bias)
    attn_low = attn_in.astype(jnp.bfloat16)
    qkv = jnp.dot(attn_low, qkv_weight, preferred_element_type=jnp.float32).astype(jnp.bfloat16)
    qkv_heads = qkv.reshape(group_count, slot_count, 3, HEADS, HDIM)
    queries = qkv_heads[:, :, 0]
    pairs = qkv_heads[:, :, 1:].reshape(group_count, 1, slot_count, 2 * model_width)
    gathered = lax.all_gather(pairs, "stream", axis=1, tiled=True)
    both_heads = gathered.reshape(group_count, 2 * slot_count, 2, HEADS, HDIM)
    key_all = both_heads[:, :, 0]
    value_all = both_heads[:, :, 1]
    slot_index = lax.broadcasted_iota(jnp.int32, (slot_count,), 0)
    patch_key = slot_index < PATCHES
    text_key = text_segment < CAPTIONS
    same_caption = text_segment[:, :, None] == text_segment[:, None, :]
    patch_part = jnp.broadcast_to(patch_key[None, None, :], (group_count, slot_count, slot_count))
    image_text = jnp.broadcast_to(text_key[:, None, :], (group_count, slot_count, slot_count))
    text_part = jnp.where(stream_index == 0, image_text, same_caption)
    visible = jnp.concatenate([patch_part, text_part], axis=2)[:, None]

    def masked_scores():
        scores = (
            jnp.einsum("gqhe,gkhe->ghqk", queries, key_all, preferred_element_type=jnp.float32)
            * score_scale
        )
        return jnp.where(visible, scores, jnp.float32(-1e30))

    scores = masked_scores()
    row_max = jnp.max(scores, axis=-1, keepdims=True)
    exp_terms = jnp.exp(scores - row_max)
    row_total = jnp.sum(exp_terms, axis=-1, keepdims=True)
    weights = exp_terms / row_total
    log_total = row_max + jnp.log(row_total)
    mixed_heads = jnp.einsum(
        "ghqk,gkhe->gqhe",
        weights.astype(jnp.bfloat16),
        value_all,
        preferred_element_type=jnp.float32,
    )
    mixed_heads = mixed_heads.astype(jnp.bfloat16).reshape(row_count, model_width)
    attn_proj = jnp.dot(mixed_heads, out_weight, preferred_element_type=jnp.float32)
    residual = flat_rows + attn_scale * attn_proj
    in_matrix = expert_in[0]
    out_matrix = expert_out[0]
    ffn_in, ln2_pull = jax.vjp(layer_norm, residual, ln2_gain[0], ln2_bias[0])
    ffn_low = ffn_in.astype(jnp.bfloat16)
    pre_act = jnp.dot(ffn_low, in_matrix, preferred_element_type=jnp.float32)
    activation = gelu_exact(pre_act).astype(jnp.bfloat16)
    ffn_out = jnp.dot(activation, out_matrix, preferred_element_type=jnp.float32)
    block_out = (residual + ffn_scale * ffn_out).astype(jnp.bfloat16)
    grad_out = out_cot.reshape(row_count, model_width).astype(jnp.float32)
    ffn_scale_grad = jnp.sum(grad_out * ffn_out, axis=0)
    grad_ffn = (ffn_scale * grad_out).astype(jnp.bfloat16)
    expert_out_grad = contract_rows(activation, grad_ffn)
    grad_act = times_transposed(grad_ffn, out_matrix)
    _, gelu_pull = jax.vjp(gelu_exact, pre_act)
    grad_pre = gelu_pull(grad_act)[0].astype(jnp.bfloat16)
    expert_in_grad = contract_rows(ffn_low, grad_pre)
    grad_ffn_in = times_transposed(grad_pre, in_matrix)
    grad_resid_norm, ln2_gain_grad, ln2_bias_grad = ln2_pull(grad_ffn_in)
    grad_resid = grad_out + grad_resid_norm
    expert_total = lax.psum((expert_in_grad, expert_out_grad, ln2_gain_grad, ln2_bias_grad), "dp")
    attn_scale_grad = jnp.sum(grad_resid * attn_proj, axis=0)
    grad_proj = (attn_scale * grad_resid).astype(jnp.bfloat16)
    out_weight_grad = contract_rows(mixed_heads, grad_proj)
    grad_mix = times_transposed(grad_proj, out_weight).astype(jnp.bfloat16)
    grad_mix = grad_mix.reshape(group_count, slot_count, HEADS, HDIM)
    weights_again = jnp.exp(masked_scores() - log_total)
    grad_probs = jnp.einsum(
        "gqhe,gkhe->ghqk", grad_mix, value_all, preferred_element_type=jnp.float32
    )
    inner_sum = jnp.sum(weights_again * grad_probs, axis=-1, keepdims=True)
    grad_scores = (weights_again * (grad_probs - inner_sum)).astype(jnp.bfloat16)
    grad_query = (
        jnp.einsum("ghqk,gkhe->gqhe", grad_scores, key_all, preferred_element_type=jnp.float32)
        * score_scale
    )
    grad_query = grad_query.astype(jnp.bfloat16).reshape(row_count, model_width)
    grad_key = (
        jnp.einsum("ghqk,gqhe->gkhe", grad_scores, queries, preferred_element_type=jnp.float32)
        * score_scale
    )
    grad_value = jnp.einsum(
        "ghqk,gqhe->gkhe",
        weights_again.astype(jnp.bfloat16),
        grad_mix,
        preferred_element_type=jnp.float32,
    )
    key_terms = jnp.stack([grad_key, grad_value], axis=2).reshape(
        group_count, 2, slot_count, 2 * model_width
    )
    owned_grads = lax.psum_scatter(
        key_terms.astype(jnp.bfloat16), "stream", scatter_dimension=1, tiled=True
    ).astype(jnp.float32)
    owned_grads = owned_grads.reshape(row_count, 2 * model_width).astype(jnp.bfloat16)
    grad_qkv = jnp.concatenate([grad_query, owned_grads], axis=1)
    qkv_weight_grad = contract_rows(attn_low, grad_qkv)
    grad_attn_in = times_transposed(grad_qkv, qkv_weight)
    grad_rows_norm, ln1_gain_grad, ln1_bias_grad = ln1_pull(grad_attn_in)
    tokens_grad = (grad_resid + grad_rows_norm).astype(jnp.bfloat16).reshape(tokens.shape)
    small_grads = jnp.stack([ln1_gain_grad, ln1_bias_grad, attn_scale_grad, ffn_scale_grad], axis=0)
    shared_total = lax.psum((qkv_weight_grad, out_weight_grad, small_grads), ("dp", "stream"))
    small_total = shared_total[2]
    return (
        block_out.reshape(tokens.shape),
        tokens_grad,
        small_total[0],
        small_total[1],
        shared_total[0],
        shared_total[1],
        small_total[2],
        small_total[3],
        expert_total[2][None, :],
        expert_total[3][None, :],
        expert_total[0][None, :, :],
        expert_total[1][None, :, :],
    )


def solution(mesh):
    placed = (
        P("dp", "stream", None, None),
        P("dp", None),
        P(),
        P(),
        P(),
        P(),
        P(),
        P(),
        P("stream", None),
        P("stream", None),
        P("stream", None, None),
        P("stream", None, None),
        P("dp", "stream", None, None),
    )
    return jax.shard_map(
        shards,
        mesh=mesh,
        in_specs=placed,
        out_specs=(
            P("dp", "stream", None, None),
            P("dp", "stream", None, None),
            P(),
            P(),
            P(),
            P(),
            P(),
            P(),
            P("stream", None),
            P("stream", None),
            P("stream", None, None),
            P("stream", None, None),
        ),
        check_vma=False,
    )
```

profile of v0, /device:TPU:0, one launch (start us, length us, event | category | flops | bytes accessed | tf_op | source)
XLA Modules:
  0.0 1063.4 jit_solution(14414983165366514719)
XLA Ops:
  17.6 5.4 convolution_convert_fusion
  23.0 6.6 copy.61
  29.6 15.1 %reshape.175 = bf16[5,200,3,12,64]{1,0,4,3,2:T(8,128)(2,1)} reshape(bf16[1000,2304]{0,1:T(8,128)(2,1)} %copy.61) | data formatting | bytes 9216000 | tf_op jit(solution)/shard_map/reshape | solution.py:61
  44.7 6.1 slice.32
  50.8 7.2 copy.63
  58.0 3.7 slice.34
  64.0 2.8 fusion.25
  66.8 72.7 %all-gather.2.cloned.1.call-done = bf16[5,2,200,1536]{3,2,0,1:T(8,128)(2,1)} async-done(((bf16[5,1,200,1536]{3,2,0,1:T(8,128)(2,1)}), bf16[5,2,200,1536]{3,2,0,1:T(8,128)(2,1)}) %all-gather.2.cloned.1.call-update) | async-done | bytes 6144016 | tf_op jit(solution)/shard_map/all_gather | solution.py:64
  139.5 20.1 %copy.64 = bf16[5,2,200,1536]{2,1,3,0:T(2,128)(2,1)} copy(bf16[5,2,200,1536]{3,2,0,1:T(8,128)(2,1)} %all-gather.2.cloned.1.call-done) | data formatting | bytes 12288000 | tf_op jit(solution)/shard_map/all_gather | solution.py:64
  159.6 13.1 %reshape.177 = bf16[5,400,2,12,64]{1,4,3,2,0:T(8,128)(2,1)} reshape(bf16[5,2,200,1536]{2,1,3,0:T(2,128)(2,1)} %copy.64) | data formatting | bytes 12288000 | tf_op jit(solution)/shard_map/reshape | solution.py:65
  172.7 15.1 %fusion.39 = (f32[5,12,200]{2,1,0:T(8,128)S(1)}, f32[5,12,200,400]{3,2,1,0:T(8,128)}) fusion(bf16[5,400,2,12,64]{1,4,3,2,0:T(8,128)(2,1)} %reshape.177, bf16[5,200,1,12,64]{1,0,4,3,2:T(8,128)(2,1)} %slice.34, pred[5,200,400]{2,1,0:T(8,128)(4,1)} %pad_add_fusion), kind=kOutput, calls=%fused_computation.101 | convolution fusion | flops 628787968 | bytes 26837888 | tf_op jit(solution)/shard_map/gqhe,gkhe->ghqk/dot_general | solution.py:79
  187.9 11.5 %fusion = f32[5,12,200]{2,1,0:T(8,128)S(1)} fusion(f32[5,12,200,400]{3,2,1,0:T(8,128)} %get-tuple-element.88, f32[5,12,200]{2,1,0:T(8,128)S(1)} %get-tuple-element.87), kind=kLoop, calls=%fused_computation.6 | loop fusion | flops 9588000 | bytes 19296000 | tf_op jit(solution)/shard_map/reduce_sum | solution.py:87
  199.4 11.2 %convert_bitcast_fusion.1 = bf16[5,200,12,64]{1,3,2,0:T(8,128)(2,1)S(1)} fusion(f32[5,12,200,400]{3,2,1,0:T(8,128)} %get-tuple-element.88, f32[5,12,200]{2,1,0:T(8,128)S(1)} %fusion, f32[5,12,200]{2,1,0:T(8,128)S(1)} %get-tuple-element.87, bf16[5,400,2,12,64]{1,4,3,2,0:T(8,128)(2,1)S(1)} %copy-done.3), kind=kOutput, calls=%fused_computation.76 | convolution fusion | flops 629568000 | bytes 24832000 | tf_op jit(solution)/shard_map/ghqk,gkhe->gqhe/dot_general | solution.py:90
  211.2 3.2 copy.68
  214.4 5.5 reshape.178
  219.9 6.3 multiply_add_fusion
  230.7 35.5 %multiply_convert_fusion.1 = (bf16[1000,3072]{1,0:T(8,128)(2,1)}, f32[1000,3072]{1,0:T(8,128)}, f32[1000,3072]{1,0:T(8,128)}) fusion(bf16[1,768,3072]{2,1,0:T(8,128)(2,1)} %param.23, f32[1000,768]{1,0:T(8,128)} %get-tuple-element.89, f32[768]{0:T(1024)S(1)} %reduce.5, f32[768]{0:T(1024)S(1)} %reduce.4, f32[1000]{0:T(1024)S(1)} %fusion.34, ...), kind=kOutput, calls=%fused_computation.13 | convolution fusion | flops 4922112000 | bytes 38524736 | tf_op jit(solution)/shard_map/dot_general | solution.py:103
  266.2 15.5 %add_convert_fusion = bf16[1000,3072]{1,0:T(8,128)(2,1)} fusion(f32[1000,3072]{1,0:T(8,128)} %get-tuple-element.81, f32[1000,3072]{1,0:T(8,128)} %get-tuple-element.91, bf16[1000,768]{1,0:T(8,128)(2,1)S(1)} %bitcast.116, bf16[1,3072,768]{2,1,0:T(8,128)(2,1)} %param.24), kind=kOutput, calls=%fused_computation.12 | convolution fusion | flops 4761600000 | bytes 36974592 | tf_op jit(solution)/shard_map/dot_general | solution.py:31
  281.8 10.3 multiply_reduce_fusion.1
  292.1 10.7 %fusion.26 = (f32[768]{0:T(1024)}, bf16[1000,768]{1,0:T(8,128)(2,1)}, f32[1000]{0:T(1024)S(1)}, f32[1000,768]{1,0:T(8,128)S(1)}, bf16[1000,768]{1,0:T(8,128)(2,1)}) fusion(bf16[5,1,200,768]{3,2,1,0:T(8,128)(2,1)S(1)} %copy-done.9, f32[1000,768]{1,0:T(8,128)S(1)} %copy-done.2, f32[768]{0:T(1024)S(1)} %copy-done.27, f32[1000]{0:T(1024)S(1)} %multiply_multiply_fusion.6, ...), kind=kOutput, calls=%fused_computation.56 | convolution fusion | flops 4730109952 | bytes 24711808 | tf_op jit(solution)/shard_map/dot_general | solution.py:105
  308.2 5.8 reshape.188
  314.0 6.0 copy.70
  320.0 22.1 %multiply_reduce_fusion = (f32[5,12,200]{2,1,0:T(8,128)S(1)}, f32[5,12,200,400]{3,2,1,0:T(8,128)}) fusion(f32[5,12,200,400]{3,2,1,0:T(8,128)} %get-tuple-element.88, f32[5,12,200]{2,1,0:T(8,128)} %log_add_fusion, bf16[5,200,12,64]{1,3,2,0:T(8,128)(2,1)} %copy.70, bf16[5,400,2,12,64]{1,4,3,2,0:T(8,128)(2,1)} %reshape.177), kind=kOutput, calls=%fused_computation.1 | convolution fusion | flops 628787968 | bytes 49804160 | tf_op jit(solution)/shard_map/gqhe,gkhe->ghqk/dot_general | solution.py:125
  342.1 12.6 %convert_bitcast_fusion = bf16[5,400,1,12,64]{1,4,3,0,2:T(8,128)(2,1)} fusion(bf16[5,200,12,64]{1,3,2,0:T(8,128)(2,1)S(1)} %copy-done.6, f32[5,12,200,400]{3,2,1,0:T(8,128)} %get-tuple-element.88, f32[5,12,200]{2,1,0:T(8,128)S(1)} %copy-done.11), kind=kOutput, calls=%fused_computation.47 | convolution fusion | flops 625536000 | bytes 23856000 | tf_op jit(solution)/shard_map/ghqk,gqhe->gkhe/dot_general | solution.py:139
  354.7 16.3 %multiply_convert_fusion = bf16[5,12,200,400]{3,2,1,0:T(8,128)(2,1)S(1)} fusion(f32[5,12,200,400]{3,2,1,0:T(8,128)} %get-tuple-element.94, f32[5,12,200,400]{3,2,1,0:T(8,128)} %get-tuple-element.88, f32[5,12,200]{2,1,0:T(8,128)S(1)} %get-tuple-element.93, f32[5,12,200]{2,1,0:T(8,128)S(1)} %copy-done.11), kind=kLoop, calls=%fused_computation | loop fusion | flops 19200000 | bytes 48096000 | tf_op jit(solution)/shard_map/convert_element_type | solution.py:129
  371.1 4.5 copy-done.1
  375.5 3.8 fusion.20
  379.4 7.4 pad_maximum_fusion
  386.8 7.5 copy.73
  394.3 13.2 %convert_element_type.107 = bf16[5,2,200,1536]{2,1,3,0:T(2,128)(2,1)} reshape(bf16[5,400,2,12,64]{1,4,3,2,0:T(8,128)(2,1)} %copy.73) | data formatting | bytes 12288000 | tf_op jit(solution)/shard_map/convert_element_type | solution.py:149
  407.4 19.6 %copy.74 = bf16[5,2,200,1536]{3,2,0,1:T(8,128)(2,1)} copy(bf16[5,2,200,1536]{2,1,3,0:T(2,128)(2,1)} %convert_element_type.107) | data formatting | bytes 12288000 | tf_op jit(solution)/shard_map/convert_element_type | solution.py:149
  427.1 11.2 %convolution_bitcast_fusion.1 = f32[1,768,3072]{2,1,0:T(8,128)} fusion(bf16[1000,3072]{1,0:T(8,128)(2,1)} %add_convert_fusion, f32[1000,768]{1,0:T(8,128)} %get-tuple-element.89, f32[768]{0:T(1024)S(1)} %reduce.5, f32[768]{0:T(1024)S(1)} %reduce.4, f32[1000]{0:T(1024)S(1)} %fusion.34, f32[1000]{0:T(1024)S(1)} %broadcast_multiply_fusion.1), kind=kOutput, calls=%fused_computation.31 | convolution fusion | flops 4722432000 | bytes 18667328 | tf_op jit(solution)/shard_map/dot_general | solution.py:25
  438.3 10.4 convolution_bitcast_fusion
  448.9 11.3 %fusion.32 = bf16[5,200,12,64]{1,3,2,0:T(8,128)(2,1)} fusion(bf16[5,12,200,400]{3,2,1,0:T(8,128)(2,1)} %copy-done.1, bf16[5,400,2,12,64]{1,4,3,2,0:T(8,128)(2,1)} %reshape.177), kind=kOutput, calls=%fused_computation.74 | convolution fusion | flops 615936000 | bytes 17756160 | tf_op jit(solution)/shard_map/ghqk,gkhe->gqhe/dot_general | solution.py:131
  460.2 6.3 copy.80
  466.6 6.1 reshape.187
  472.6 5.1 fusion.33
  477.8 25.0 %reduce-scatter.2.cloned.1.call-done = bf16[5,1,200,1536]{3,2,0,1:T(8,128)(2,1)} async-done(((bf16[5,2,200,1536]{3,2,0,1:T(8,128)(2,1)}), bf16[5,1,200,1536]{3,2,0,1:T(8,128)(2,1)}) %reduce-scatter.2.cloned.1.call-update) | async-done | bytes 3072016 | tf_op jit(solution)/shard_map/reduce_scatter | solution.py:148
  502.7 9.6 fusion.28
  516.9 36.8 %all-reduce.1 = (f32[1,768]{1,0:T(1,128)}, f32[1,768]{1,0:T(1,128)}) all-reduce(f32[1,768]{1,0:T(1,128)} %broadcast_in_dim.76, f32[1,768]{1,0:T(1,128)} %broadcast_in_dim.77), channel_id=1, replica_groups=mesh['dp'=16,'stream'=2] {'dp'}, use_global_device_ids=true, to_apply=%region_20.21 | all-reduce | flops 1536 | bytes 12288 | tf_op jit(solution)/shard_map/psum | solution.py:118
  553.7 7.9 multiply_reduce_fusion.3
  568.7 38.9 %psum.49 = f32[4,768]{1,0:T(4,128)S(1)} all-reduce(f32[4,768]{1,0:T(4,128)} %pad_maximum_fusion.4), channel_id=1, replica_groups=mesh['dp'=16,'stream'=2] {'dp','stream'}, use_global_device_ids=true, to_apply=%region_16.17 | all-reduce | flops 3072 | bytes 24576 | tf_op jit(solution)/shard_map/psum | solution.py:158
  608.2 4.3 add_convert_fusion.1
  612.5 225.5 %all-reduce.8.cloned.1.call-done = (f32[1,768,3072]{2,1,0:T(8,128)}, f32[1,3072,768]{2,1,0:T(8,128)}) async-done(((f32[1,768,3072]{2,1,0:T(8,128)}, f32[1,3072,768]{2,1,0:T(8,128)}), (f32[1,768,3072]{2,1,0:T(8,128)}, f32[1,3072,768]{2,1,0:T(8,128)})) %all-reduce.8.cloned.1.call-update) | async-done | bytes 18874384 | tf_op jit(solution)/shard_map/psum | solution.py:118
  838.0 197.6 %all-reduce.6.cloned.1.call-done = (f32[768,2304]{1,0:T(8,128)}, f32[768,768]{1,0:T(8,128)}) async-done(((f32[768,2304]{1,0:T(8,128)}, f32[768,768]{1,0:T(8,128)}), (f32[768,2304]{1,0:T(8,128)}, f32[768,768]{1,0:T(8,128)})) %all-reduce.6.cloned.1.call-update) | async-done | bytes 9437200 | tf_op jit(solution)/shard_map/psum | solution.py:158
  1035.6 6.6 copy.96
  1043.6 9.3 copy.98
  1052.9 3.7 copy.99
  (113 shorter events, 37.3 us)
Async XLA Ops:
  7.2 10.5 copy-start
  7.2 132.3 %all-gather.2.cloned.1.call-start = ((), (), s32[]{:S(2)}) async-start(), calls=%async_computation.1 | async-start | bytes 9216000 | tf_op jit(solution)/shard_map/all_gather | solution.py:64
  11.7 11.3 %copy-start.16 = (f32[1000]{0:T(1024)}, f32[1000]{0:T(1024)S(1)}, u32[]{:S(2)}) copy-start(f32[1000]{0:T(1024)S(1)} %div.47) | copy-start | bytes 12004
  13.8 9.2 copy-start.20
  13.8 0.6 copy-start.18
  16.5 1.2 copy-start.12
  57.9 3.8 copy-start.28
  57.9 4.5 copy-start.15
  58.0 444.8 %reduce-scatter.2.cloned.1.call-start = ((), (), s32[]{:S(2)}) async-start(), calls=%async_computation.2 | async-start | bytes 9216000 | tf_op jit(solution)/shard_map/reduce_scatter | solution.py:148
  187.9 11.5 %copy-start.3 = (bf16[5,400,2,12,64]{1,4,3,2,0:T(8,128)(2,1)S(1)}, bf16[5,400,2,12,64]{1,4,3,2,0:T(8,128)(2,1)}, u32[]{:S(2)}) copy-start(bf16[5,400,2,12,64]{1,4,3,2,0:T(8,128)(2,1)} %reshape.177) | copy-start | bytes 18432004
  211.2 8.7 copy-start.22
  230.7 35.5 %copy-start.13 = (bf16[5,1,200,768]{3,2,1,0:T(8,128)(2,1)S(1)}, bf16[5,1,200,768]{3,2,1,0:T(8,128)(2,1)}, u32[]{:S(2)}) copy-start(bf16[5,1,200,768]{3,2,1,0:T(8,128)(2,1)} %fusion.25) | copy-start | bytes 4608004
  266.2 15.5 %copy-start.2 = (f32[1000,768]{1,0:T(8,128)S(1)}, f32[1000,768]{1,0:T(8,128)}, u32[]{:S(2)}) copy-start(f32[1000,768]{1,0:T(8,128)} %get-tuple-element.89) | copy-start | bytes 9216004
  281.7 10.3 copy-start.9
  281.7 10.3 copy-start.27
  281.7 10.3 copy-start.29
  292.1 10.7 %copy-start.5 = (f32[1000,768]{1,0:T(8,128)S(1)}, f32[1000,768]{1,0:T(8,128)}, u32[]{:S(2)}) copy-start(f32[1000,768]{1,0:T(8,128)} %get-tuple-element.90) | copy-start | bytes 9216004
  302.7 2.9 copy-start.14
  302.7 2.9 copy-start.23
  304.0 1.6 copy-start.8
  320.0 22.1 %copy-start.6 = (bf16[5,200,12,64]{1,3,2,0:T(8,128)(2,1)S(1)}, bf16[5,200,12,64]{1,3,2,0:T(8,128)(2,1)}, u32[]{:S(2)}) copy-start(bf16[5,200,12,64]{1,3,2,0:T(8,128)(2,1)} %copy.70) | copy-start | bytes 4608004
  320.0 22.1 %copy-start.11 = (f32[5,12,200]{2,1,0:T(8,128)S(1)}, f32[5,12,200]{2,1,0:T(8,128)}, u32[]{:S(2)}) copy-start(f32[5,12,200]{2,1,0:T(8,128)} %log_add_fusion) | copy-start | bytes 144004
  354.7 20.8 %copy-start.7 = (bf16[5,200,1,12,64]{1,0,4,3,2:T(8,128)(2,1)S(1)}, bf16[5,200,1,12,64]{1,0,4,3,2:T(8,128)(2,1)}, u32[]{:S(2)}) copy-start(bf16[5,200,1,12,64]{1,0,4,3,2:T(8,128)(2,1)} %slice.34) | copy-start | bytes 4608004
  371.1 4.5 copy-start.1
  427.0 411.0 %all-reduce.8.cloned.1.call-start = ((), (), s32[]{:S(2)}) async-start(), calls=%async_computation.4 | async-start | bytes 37748736 | tf_op jit(solution)/shard_map/psum | solution.py:118
  427.1 11.2 %copy-start.30 = (bf16[1000,768]{1,0:T(8,128)(2,1)S(1)}, bf16[1000,768]{1,0:T(8,128)(2,1)}, u32[]{:S(2)}) copy-start(bf16[1000,768]{1,0:T(8,128)(2,1)} %get-tuple-element.86) | copy-start | bytes 4608004
  448.7 586.9 %all-reduce.6.cloned.1.call-start = ((), (), s32[]{:S(2)}) async-start(), calls=%async_computation.3 | async-start | bytes 18874368 | tf_op jit(solution)/shard_map/psum | solution.py:158
  466.6 6.1 copy-start.24
  512.4 2.6 copy-start.26
  512.4 41.3 %copy-start.17 = (f32[1000]{0:T(1024)S(1)}, f32[1000]{0:T(1024)}, u32[]{:S(2)}) copy-start(f32[1000]{0:T(1024)} %copy-done.16) | copy-start | bytes 12004
  512.4 41.3 %copy-start.19 = (f32[1000]{0:T(1024)S(1)}, f32[1000]{0:T(1024)}, u32[]{:S(2)}) copy-start(f32[1000]{0:T(1024)} %copy-done.18) | copy-start | bytes 12004
  512.4 41.3 %copy-start.25 = (f32[768]{0:T(1024)S(1)}, f32[768]{0:T(1024)}, u32[]{:S(2)}) copy-start(f32[768]{0:T(1024)} %param.15) | copy-start | bytes 9220
  553.6 9.0 copy-start.21
  553.6 9.1 copy-start.4
  1035.6 6.6 copy-start.10
  1042.2 10.7 %slice-start = ((s8[9437184]{0:T(1024)(128)(4,1)}), s8[4194304]{0:T(1024)(128)(4,1)S(1)}, s32[]{:S(2)}) async-start(s8[9437184]{0:T(1024)(128)(4,1)} %bitcast.114), calls=%async_computation.5 | async-start | bytes 8388608
  1043.6 9.3 slice-start.1
  1043.6 9.3 slice-start.2
Sparse Core Ops, SparseCore 0:
  58.1 81.4 all-gather.1
  427.2 75.5 reduce-scatter.1
  507.4 330.5 all-reduce.7
  844.4 191.1 all-reduce.5
where the time goes:
time: 1070 us; the launch traced here: 1060 us
  waiting for transfers between devices  521 us (49%)
  matrix products  207 us (19%)
  local copies, waits for them, and re-layouts  181 us (17%)
  blocking collectives  75.6 us (7%)
  other arithmetic  64.7 us (6%)
  between operations  14.3 us (1%)
    psum x1, waiting for transfers between devices, shards(): lax.psum((expert_in_grad, expert_out_grad, ln2_gain_grad, ln2_bias_grad),...  226 us
    psum x1, waiting for transfers between devices, shards(): lax.psum((qkv_weight_grad, out_weight_grad, small_grads), ('dp', 'stream'))  198 us
    all_gather x1, waiting for transfers between devices, shards(): gathered = lax.all_gather(pairs, 'stream', axis=1, tiled=True)  72.7 us
    psum x1, blocking collectives, shards(): lax.psum((qkv_weight_grad, out_weight_grad, small_grads), ('dp', 'stream'))  38.9 us
    psum x1, blocking collectives, shards(): lax.psum((expert_in_grad, expert_out_grad, ln2_gain_grad, ln2_bias_grad),...  36.8 us
    dot_general x4, matrix products, contract_rows(): lax.dot_general(left_side, right_side, (((0,), (0,)), ((), ())), preferre...  36.4 us
    dot_general x4, matrix products, times_transposed(): lax.dot_general(left_side, right_side, (((1,), (1,)), ((), ())), preferre...  36.2 us
    dot_general x1, matrix products, shards(): pre_act = jnp.dot(ffn_low, in_matrix, preferred_element_type=jnp.float32)  35.5 us
  transfers between devices with their start and end apart: 4, of which 4 were waited for; matrix products, arithmetic and copies ran while one was open for 9% of the time, Pallas kernels for 0%

commit v1 on v0

--- a/solution.py
+++ b/solution.py
@@ -61,7 +61,10 @@
     qkv_heads = qkv.reshape(group_count, slot_count, 3, HEADS, HDIM)
     queries = qkv_heads[:, :, 0]
     pairs = qkv_heads[:, :, 1:].reshape(group_count, 1, slot_count, 2 * model_width)
-    gathered = lax.all_gather(pairs, "stream", axis=1, tiled=True)
+    gathered = jnp.concatenate(
+        lax.all_to_all(jnp.stack([pairs for _ in range(lax.psum(1, "stream"))], 0), "stream", 0, 0),
+        1,
+    )
     both_heads = gathered.reshape(group_count, 2 * slot_count, 2, HEADS, HDIM)
     key_all = both_heads[:, :, 0]
     value_all = both_heads[:, :, 1]

time: 1070 us -> 1010 us (0.944)
  waiting for transfers between devices: 521 us -> 449 us
    all_gather x1 -> x0, waiting for transfers between devices: 72.7 us -> none  [shards(): gathered = lax.all_gather(pairs, 'stream', axis=1, tiled=True)]
    all_to_all x0 -> x1, waiting for transfers between devices: none -> 61 us  [shards(): lax.all_to_all(jnp.stack([pairs for _ in range(lax.psum(1, 'stream'))], 0...]
    psum x1, waiting for transfers between devices: 226 us -> 165 us  [shards(): lax.psum((expert_in_grad, expert_out_grad, ln2_gain_grad, ln2_bias_grad),...]
    another operation x0 -> x2, local copies, waits for them, and re-layouts: none -> 22.8 us  [the longest x1 13.1 us: shards(): both_heads = gathered.reshape(group_count, 2 * slot_count, 2, HEADS, HDIM)]
    all_gather x1 -> x0, local copies, waits for them, and re-layouts: 20.1 us -> none  [shards(): gathered = lax.all_gather(pairs, 'stream', axis=1, tiled=True)]
where the time goes in v1:
time: 1010 us; the launch traced here: 1000 us
  waiting for transfers between devices  449 us (44%)
  matrix products  207 us (20%)
  local copies, waits for them, and re-layouts  181 us (18%)
  blocking collectives  75.7 us (7%)
  other arithmetic  69.5 us (7%)
  between operations  16.1 us (2%)
    psum x1, waiting for transfers between devices, shards(): lax.psum((qkv_weight_grad, out_weight_grad, small_grads), ('dp', 'stream'))  197 us
    psum x1, waiting for transfers between devices, shards(): lax.psum((expert_in_grad, expert_out_grad, ln2_gain_grad, ln2_bias_grad),...  165 us
    all_to_all x1, waiting for transfers between devices, shards(): lax.all_to_all(jnp.stack([pairs for _ in range(lax.psum(1, 'stream'))], 0...  61 us
    psum x1, blocking collectives, shards(): lax.psum((qkv_weight_grad, out_weight_grad, small_grads), ('dp', 'stream'))  38.9 us
    psum x1, blocking collectives, shards(): lax.psum((expert_in_grad, expert_out_grad, ln2_gain_grad, ln2_bias_grad),...  36.7 us
    dot_general x4, matrix products, contract_rows(): lax.dot_general(left_side, right_side, (((0,), (0,)), ((), ())), preferre...  36.5 us
    dot_general x4, matrix products, times_transposed(): lax.dot_general(left_side, right_side, (((1,), (1,)), ((), ())), preferre...  36.2 us
    dot_general x1, matrix products, shards(): pre_act = jnp.dot(ffn_low, in_matrix, preferred_element_type=jnp.float32)  35.5 us
  transfers between devices with their start and end apart: 4, of which 4 were waited for; matrix products, arithmetic and copies ran while one was open for 9% of the time, Pallas kernels for 0%

profile of v1, /device:TPU:0, one launch (start us, length us, event | category | flops | bytes accessed | tf_op | source)
XLA Modules:
  0.0 1004.6 jit_solution(10668912749533286006)
XLA Ops:
  18.4 5.3 convolution_convert_fusion
  23.8 6.6 copy.61
  30.4 15.1 %reshape.172 = bf16[5,200,3,12,64]{1,0,4,3,2:T(8,128)(2,1)} reshape(bf16[1000,2304]{0,1:T(8,128)(2,1)} %copy.61) | data formatting | bytes 9216000 | tf_op jit(solution)/shard_map/reshape | solution.py:61
  49.3 4.7 pad_maximum_fusion
  54.0 9.7 copy.63
  63.7 6.2 all-to-all-start
  70.0 3.7 slice.34
  78.8 61.0 %all-to-all-done = bf16[2,5,1,200,1536]{4,3,2,1,0:T(8,128)(2,1)} async-done(((bf16[2,5,1,200,1536]{4,3,2,1,0:T(8,128)(2,1)}), bf16[2,5,1,200,1536]{4,3,2,1,0:T(8,128)(2,1)}, u32[]{:S(2)}, u32[]{:S(2)}) %all-to-all-start) | async-done | bytes 6144032 | tf_op jit(solution)/shard_map/all_to_all | solution.py:65
  139.8 20.1 %copy.64 = bf16[5,2,1,200,1536]{3,1,4,0,2:T(2,128)(2,1)} copy(bf16[5,2,1,200,1536]{4,3,2,0,1:T(8,128)(2,1)} %bitcast.2) | data formatting | bytes 12288000 | tf_op jit(solution)/shard_map/reshape | solution.py:64
  159.9 13.1 %reshape_reshape.3 = bf16[5,400,2,12,64]{1,4,3,2,0:T(8,128)(2,1)} reshape(bf16[5,2,1,200,1536]{3,1,4,0,2:T(2,128)(2,1)} %copy.64) | data formatting | bytes 12288000 | tf_op jit(solution)/shard_map/reshape;reshape | solution.py:68
  173.0 15.1 %fusion.39 = (f32[5,12,200]{2,1,0:T(8,128)S(1)}, f32[5,12,200,400]{3,2,1,0:T(8,128)}) fusion(bf16[5,400,2,12,64]{1,4,3,2,0:T(8,128)(2,1)} %reshape_reshape.3, bf16[5,200,1,12,64]{1,0,4,3,2:T(8,128)(2,1)} %slice.34, pred[5,200,400]{2,1,0:T(8,128)(4,1)} %pad_add_fusion), kind=kOutput, calls=%fused_computation.102 | convolution fusion | flops 628787968 | bytes 26837888 | tf_op jit(solution)/shard_map/gqhe,gkhe->ghqk/dot_general | solution.py:82
  188.1 11.5 %fusion = f32[5,12,200]{2,1,0:T(8,128)S(1)} fusion(f32[5,12,200,400]{3,2,1,0:T(8,128)} %get-tuple-element.88, f32[5,12,200]{2,1,0:T(8,128)S(1)} %get-tuple-element.87), kind=kLoop, calls=%fused_computation.6 | loop fusion | flops 9588000 | bytes 19296000 | tf_op jit(solution)/shard_map/reduce_sum | solution.py:90
  199.7 11.2 %convert_bitcast_fusion.1 = bf16[5,200,12,64]{1,3,2,0:T(8,128)(2,1)S(1)} fusion(f32[5,12,200,400]{3,2,1,0:T(8,128)} %get-tuple-element.88, f32[5,12,200]{2,1,0:T(8,128)S(1)} %fusion, f32[5,12,200]{2,1,0:T(8,128)S(1)} %get-tuple-element.87, bf16[5,400,2,12,64]{1,4,3,2,0:T(8,128)(2,1)S(1)} %copy-done.3), kind=kOutput, calls=%fused_computation.77 | convolution fusion | flops 629568000 | bytes 24832000 | tf_op jit(solution)/shard_map/ghqk,gkhe->gqhe/dot_general | solution.py:93
  211.5 3.2 copy.68
  214.7 5.5 reshape.174
  220.2 6.3 multiply_add_fusion
  231.0 35.5 %multiply_convert_fusion.1 = (bf16[1000,3072]{1,0:T(8,128)(2,1)}, f32[1000,3072]{1,0:T(8,128)}, f32[1000,3072]{1,0:T(8,128)}) fusion(bf16[1,768,3072]{2,1,0:T(8,128)(2,1)} %param.23, f32[1000,768]{1,0:T(8,128)} %get-tuple-element.89, f32[768]{0:T(1024)S(1)} %reduce.5, f32[768]{0:T(1024)S(1)} %reduce.4, f32[1000]{0:T(1024)S(1)} %fusion.34, ...), kind=kOutput, calls=%fused_computation.13 | convolution fusion | flops 4922112000 | bytes 38524736 | tf_op jit(solution)/shard_map/dot_general | solution.py:106
  266.5 15.5 %add_convert_fusion = bf16[1000,3072]{1,0:T(8,128)(2,1)} fusion(f32[1000,3072]{1,0:T(8,128)} %get-tuple-element.81, f32[1000,3072]{1,0:T(8,128)} %get-tuple-element.91, bf16[1000,768]{1,0:T(8,128)(2,1)S(1)} %bitcast.117, bf16[1,3072,768]{2,1,0:T(8,128)(2,1)} %param.24), kind=kOutput, calls=%fused_computation.12 | convolution fusion | flops 4761600000 | bytes 36974592 | tf_op jit(solution)/shard_map/dot_general | solution.py:31
  282.0 10.3 %multiply_reduce_fusion.1 = (f32[768]{0:T(1024)}, f32[1000]{0:T(1024)S(1)}, f32[768]{0:T(1024)}, f32[1000,768]{1,0:T(8,128)S(1)}) fusion(f32[1000,768]{1,0:T(8,128)S(1)} %copy-done.2, f32[1000]{0:T(1024)S(1)} %fusion.34, f32[1000]{0:T(1024)S(1)} %broadcast_multiply_fusion.1, f32[768]{0:T(1024)S(1)} %reduce.4, bf16[1000,3072]{1,0:T(8,128)(2,1)} %add_convert_fusion, ...), kind=kOutput, calls=%fused_computation.59 | convolution fusion | flops 4724732928 | bytes 17027808 | tf_op jit(solution)/shard_map/dot_general | solution.py:31
  292.4 10.7 %fusion.26 = (f32[768]{0:T(1024)}, bf16[1000,768]{1,0:T(8,128)(2,1)}, f32[1000]{0:T(1024)S(1)}, f32[1000,768]{1,0:T(8,128)S(1)}, bf16[1000,768]{1,0:T(8,128)(2,1)}) fusion(bf16[5,1,200,768]{3,2,1,0:T(8,128)(2,1)S(1)} %copy-done.9, f32[1000,768]{1,0:T(8,128)S(1)} %copy-done.2, f32[768]{0:T(1024)S(1)} %copy-done.27, f32[1000]{0:T(1024)S(1)} %multiply_multiply_fusion.6, ...), kind=kOutput, calls=%fused_computation.57 | convolution fusion | flops 4730109952 | bytes 24711808 | tf_op jit(solution)/shard_map/dot_general | solution.py:108
  308.5 5.8 reshape.184
  314.3 6.0 copy.70
  320.3 22.1 %multiply_reduce_fusion = (f32[5,12,200]{2,1,0:T(8,128)S(1)}, f32[5,12,200,400]{3,2,1,0:T(8,128)}) fusion(f32[5,12,200,400]{3,2,1,0:T(8,128)} %get-tuple-element.88, f32[5,12,200]{2,1,0:T(8,128)} %log_add_fusion, bf16[5,200,12,64]{1,3,2,0:T(8,128)(2,1)} %copy.70, bf16[5,400,2,12,64]{1,4,3,2,0:T(8,128)(2,1)} %reshape_reshape.3), kind=kOutput, calls=%fused_computation.1 | convolution fusion | flops 628787968 | bytes 49804160 | tf_op jit(solution)/shard_map/gqhe,gkhe->ghqk/dot_general | solution.py:128
  342.4 12.6 %convert_bitcast_fusion = bf16[5,400,1,12,64]{1,4,3,0,2:T(8,128)(2,1)} fusion(bf16[5,200,12,64]{1,3,2,0:T(8,128)(2,1)S(1)} %copy-done.6, f32[5,12,200,400]{3,2,1,0:T(8,128)} %get-tuple-element.88, f32[5,12,200]{2,1,0:T(8,128)S(1)} %copy-done.11), kind=kOutput, calls=%fused_computation.48 | convolution fusion | flops 625536000 | bytes 23856000 | tf_op jit(solution)/shard_map/ghqk,gqhe->gkhe/dot_general | solution.py:142
  355.0 16.3 %multiply_convert_fusion = bf16[5,12,200,400]{3,2,1,0:T(8,128)(2,1)S(1)} fusion(f32[5,12,200,400]{3,2,1,0:T(8,128)} %get-tuple-element.94, f32[5,12,200,400]{3,2,1,0:T(8,128)} %get-tuple-element.88, f32[5,12,200]{2,1,0:T(8,128)S(1)} %get-tuple-element.93, f32[5,12,200]{2,1,0:T(8,128)S(1)} %copy-done.11), kind=kLoop, calls=%fused_computation | loop fusion | flops 19200000 | bytes 48096000 | tf_op jit(solution)/shard_map/convert_element_type | solution.py:132
  371.4 4.5 copy-done.1
  375.8 3.8 fusion.20
  379.7 7.4 pad_maximum_fusion.1
  387.1 7.5 copy.73
  394.6 13.2 %convert_element_type.107 = bf16[5,2,200,1536]{2,1,3,0:T(2,128)(2,1)} reshape(bf16[5,400,2,12,64]{1,4,3,2,0:T(8,128)(2,1)} %copy.73) | data formatting | bytes 12288000 | tf_op jit(solution)/shard_map/convert_element_type | solution.py:152
  407.7 19.6 %copy.74 = bf16[5,2,200,1536]{3,2,0,1:T(8,128)(2,1)} copy(bf16[5,2,200,1536]{2,1,3,0:T(2,128)(2,1)} %convert_element_type.107) | data formatting | bytes 12288000 | tf_op jit(solution)/shard_map/convert_element_type | solution.py:152
  427.4 11.2 %convolution_bitcast_fusion.1 = f32[1,768,3072]{2,1,0:T(8,128)} fusion(bf16[1000,3072]{1,0:T(8,128)(2,1)} %add_convert_fusion, f32[1000,768]{1,0:T(8,128)} %get-tuple-element.89, f32[768]{0:T(1024)S(1)} %reduce.5, f32[768]{0:T(1024)S(1)} %reduce.4, f32[1000]{0:T(1024)S(1)} %fusion.34, f32[1000]{0:T(1024)S(1)} %broadcast_multiply_fusion.1), kind=kOutput, calls=%fused_computation.32 | convolution fusion | flops 4722432000 | bytes 18667328 | tf_op jit(solution)/shard_map/dot_general | solution.py:25
  438.6 10.4 %convolution_bitcast_fusion = f32[1,3072,768]{2,1,0:T(8,128)} fusion(bf16[1000,3072]{1,0:T(8,128)(2,1)} %get-tuple-element.80, bf16[1000,768]{1,0:T(8,128)(2,1)S(1)} %copy-done.30), kind=kOutput, calls=%fused_computation.31 | convolution fusion | flops 4718592000 | bytes 17117184 | tf_op jit(solution)/shard_map/dot_general | solution.py:25
  449.2 11.3 %fusion.32 = bf16[5,200,12,64]{1,3,2,0:T(8,128)(2,1)} fusion(bf16[5,12,200,400]{3,2,1,0:T(8,128)(2,1)} %copy-done.1, bf16[5,400,2,12,64]{1,4,3,2,0:T(8,128)(2,1)} %reshape_reshape.3), kind=kOutput, calls=%fused_computation.75 | convolution fusion | flops 615936000 | bytes 17756160 | tf_op jit(solution)/shard_map/ghqk,gkhe->gqhe/dot_general | solution.py:134
  460.6 6.4 copy.78
  467.0 6.2 reshape.183
  473.2 5.2 fusion.33
  478.3 25.1 %reduce-scatter.2.cloned.1.call-done = bf16[5,1,200,1536]{3,2,0,1:T(8,128)(2,1)} async-done(((bf16[5,2,200,1536]{3,2,0,1:T(8,128)(2,1)}), bf16[5,1,200,1536]{3,2,0,1:T(8,128)(2,1)}) %reduce-scatter.2.cloned.1.call-update) | async-done | bytes 3072016 | tf_op jit(solution)/shard_map/reduce_scatter | solution.py:151
  503.5 9.8 fusion.28
  517.7 36.7 %all-reduce.1 = (f32[1,768]{1,0:T(1,128)}, f32[1,768]{1,0:T(1,128)}) all-reduce(f32[1,768]{1,0:T(1,128)} %broadcast_in_dim.76, f32[1,768]{1,0:T(1,128)} %broadcast_in_dim.77), channel_id=1, replica_groups=mesh['dp'=16,'stream'=2] {'dp'}, use_global_device_ids=true, to_apply=%region_20.21 | all-reduce | flops 1536 | bytes 12288 | tf_op jit(solution)/shard_map/psum | solution.py:121
  554.5 7.9 multiply_reduce_fusion.3
  569.6 38.9 %psum.49 = f32[4,768]{1,0:T(4,128)S(1)} all-reduce(f32[4,768]{1,0:T(4,128)} %pad_maximum_fusion.5), channel_id=1, replica_groups=mesh['dp'=16,'stream'=2] {'dp','stream'}, use_global_device_ids=true, to_apply=%region_16.17 | all-reduce | flops 3072 | bytes 24576 | tf_op jit(solution)/shard_map/psum | solution.py:161
  609.1 4.3 add_convert_fusion.1
  613.4 165.4 %all-reduce.8.cloned.1.call-done = (f32[1,768,3072]{2,1,0:T(8,128)}, f32[1,3072,768]{2,1,0:T(8,128)}) async-done(((f32[1,768,3072]{2,1,0:T(8,128)}, f32[1,3072,768]{2,1,0:T(8,128)}), (f32[1,768,3072]{2,1,0:T(8,128)}, f32[1,3072,768]{2,1,0:T(8,128)})) %all-reduce.8.cloned.1.call-update) | async-done | bytes 18874384 | tf_op jit(solution)/shard_map/psum | solution.py:121
  778.8 197.0 %all-reduce.6.cloned.1.call-done = (f32[768,2304]{1,0:T(8,128)}, f32[768,768]{1,0:T(8,128)}) async-done(((f32[768,2304]{1,0:T(8,128)}, f32[768,768]{1,0:T(8,128)}), (f32[768,2304]{1,0:T(8,128)}, f32[768,768]{1,0:T(8,128)})) %all-reduce.6.cloned.1.call-update) | async-done | bytes 9437200 | tf_op jit(solution)/shard_map/psum | solution.py:161
  975.9 6.6 copy.94
  983.9 9.3 copy.96
  993.2 3.7 copy.97
  (115 shorter events, 44.0 us)
Async XLA Ops:
  8.0 10.4 %copy-start = (bf16[768,2304]{1,0:T(8,128)(2,1)S(1)}, bf16[768,2304]{1,0:T(8,128)(2,1)}, u32[]{:S(2)}) copy-start(bf16[768,2304]{1,0:T(8,128)(2,1)} %param.17) | copy-start | bytes 10616836
  12.5 11.3 %copy-start.16 = (f32[1000]{0:T(1024)}, f32[1000]{0:T(1024)S(1)}, u32[]{:S(2)}) copy-start(f32[1000]{0:T(1024)S(1)} %div.47) | copy-start | bytes 12004
  14.6 9.2 copy-start.20
  14.6 0.6 copy-start.18
  17.3 1.2 copy-start.12
  45.5 2.8 slice-start
  63.7 76.1 %all-to-all-start = ((bf16[2,5,1,200,1536]{4,3,2,1,0:T(8,128)(2,1)}), bf16[2,5,1,200,1536]{4,3,2,1,0:T(8,128)(2,1)}, u32[]{:S(2)}, u32[]{:S(2)}) async-start(bf16[2,5,1,200,1536]{4,3,2,1,0:T(8,128)(2,1)} %copy.63), calls=%async_computation | async-start | bytes 12288000 | tf_op jit(solution)/shard_map/all_to_all | solution.py:65
  70.0 3.8 copy-start.28
  70.0 4.5 copy-start.15
  70.0 433.5 %reduce-scatter.2.cloned.1.call-start = ((), (), s32[]{:S(2)}) async-start(), calls=%async_computation.2 | async-start | bytes 9216000 | tf_op jit(solution)/shard_map/reduce_scatter | solution.py:151
  188.1 11.5 %copy-start.3 = (bf16[5,400,2,12,64]{1,4,3,2,0:T(8,128)(2,1)S(1)}, bf16[5,400,2,12,64]{1,4,3,2,0:T(8,128)(2,1)}, u32[]{:S(2)}) copy-start(bf16[5,400,2,12,64]{1,4,3,2,0:T(8,128)(2,1)} %reshape_reshape.3) | copy-start | bytes 18432004
  211.5 8.7 copy-start.22
  231.0 35.5 %copy-start.13 = (bf16[5,1,200,768]{3,2,1,0:T(8,128)(2,1)S(1)}, bf16[5,1,200,768]{3,2,1,0:T(8,128)(2,1)}, u32[]{:S(2)}) copy-start(bf16[5,1,200,768]{3,2,1,0:T(8,128)(2,1)} %fusion.25) | copy-start | bytes 4608004
  266.5 15.5 %copy-start.2 = (f32[1000,768]{1,0:T(8,128)S(1)}, f32[1000,768]{1,0:T(8,128)}, u32[]{:S(2)}) copy-start(f32[1000,768]{1,0:T(8,128)} %get-tuple-element.89) | copy-start | bytes 9216004
  282.0 10.3 %copy-start.9 = (bf16[5,1,200,768]{3,2,1,0:T(8,128)(2,1)S(1)}, bf16[5,1,200,768]{3,2,1,0:T(8,128)(2,1)}, u32[]{:S(2)}) copy-start(bf16[5,1,200,768]{3,2,1,0:T(8,128)(2,1)} %param.25) | copy-start | bytes 4608004
  282.0 10.3 %copy-start.27 = (f32[768]{0:T(1024)S(1)}, f32[768]{0:T(1024)}, u32[]{:S(2)}) copy-start(f32[768]{0:T(1024)} %param.20) | copy-start | bytes 9220
  282.0 10.3 %copy-start.29 = (bf16[1000,3072]{1,0:T(8,128)(2,1)S(1)}, bf16[1000,3072]{1,0:T(8,128)(2,1)}, u32[]{:S(2)}) copy-start(bf16[1000,3072]{1,0:T(8,128)(2,1)} %get-tuple-element.80) | copy-start | bytes 18432004
  292.3 10.7 %copy-start.5 = (f32[1000,768]{1,0:T(8,128)S(1)}, f32[1000,768]{1,0:T(8,128)}, u32[]{:S(2)}) copy-start(f32[1000,768]{1,0:T(8,128)} %get-tuple-element.90) | copy-start | bytes 9216004
  303.0 2.9 copy-start.14
  303.0 2.9 copy-start.23
  304.3 1.6 copy-start.8
  320.3 22.1 %copy-start.6 = (bf16[5,200,12,64]{1,3,2,0:T(8,128)(2,1)S(1)}, bf16[5,200,12,64]{1,3,2,0:T(8,128)(2,1)}, u32[]{:S(2)}) copy-start(bf16[5,200,12,64]{1,3,2,0:T(8,128)(2,1)} %copy.70) | copy-start | bytes 4608004
  320.3 22.1 %copy-start.11 = (f32[5,12,200]{2,1,0:T(8,128)S(1)}, f32[5,12,200]{2,1,0:T(8,128)}, u32[]{:S(2)}) copy-start(f32[5,12,200]{2,1,0:T(8,128)} %log_add_fusion) | copy-start | bytes 144004
  355.0 20.8 %copy-start.7 = (bf16[5,200,1,12,64]{1,0,4,3,2:T(8,128)(2,1)S(1)}, bf16[5,200,1,12,64]{1,0,4,3,2:T(8,128)(2,1)}, u32[]{:S(2)}) copy-start(bf16[5,200,1,12,64]{1,0,4,3,2:T(8,128)(2,1)} %slice.34) | copy-start | bytes 4608004
  371.3 4.5 copy-start.1
  427.3 351.5 %all-reduce.8.cloned.1.call-start = ((), (), s32[]{:S(2)}) async-start(), calls=%async_computation.4 | async-start | bytes 37748736 | tf_op jit(solution)/shard_map/psum | solution.py:121
  427.4 11.2 %copy-start.30 = (bf16[1000,768]{1,0:T(8,128)(2,1)S(1)}, bf16[1000,768]{1,0:T(8,128)(2,1)}, u32[]{:S(2)}) copy-start(bf16[1000,768]{1,0:T(8,128)(2,1)} %get-tuple-element.86) | copy-start | bytes 4608004
  449.0 526.9 %all-reduce.6.cloned.1.call-start = ((), (), s32[]{:S(2)}) async-start(), calls=%async_computation.3 | async-start | bytes 18874368 | tf_op jit(solution)/shard_map/psum | solution.py:161
  460.6 12.6 %copy-start.24 = (f32[768]{0:T(1024)S(1)}, f32[768]{0:T(1024)}, u32[]{:S(2)}) copy-start(f32[768]{0:T(1024)} %param.19) | copy-start | bytes 9220
  513.2 2.6 copy-start.26
  513.2 41.2 %copy-start.17 = (f32[1000]{0:T(1024)S(1)}, f32[1000]{0:T(1024)}, u32[]{:S(2)}) copy-start(f32[1000]{0:T(1024)} %copy-done.16) | copy-start | bytes 12004
  513.3 41.2 %copy-start.19 = (f32[1000]{0:T(1024)S(1)}, f32[1000]{0:T(1024)}, u32[]{:S(2)}) copy-start(f32[1000]{0:T(1024)} %copy-done.18) | copy-start | bytes 12004
  513.3 41.2 %copy-start.25 = (f32[768]{0:T(1024)S(1)}, f32[768]{0:T(1024)}, u32[]{:S(2)}) copy-start(f32[768]{0:T(1024)} %param.15) | copy-start | bytes 9220
  554.5 9.0 copy-start.21
  554.5 9.1 copy-start.4
  975.9 6.6 copy-start.10
  982.5 10.7 %slice-start.1 = ((s8[9437184]{0:T(1024)(128)(4,1)}), s8[4194304]{0:T(1024)(128)(4,1)S(1)}, s32[]{:S(2)}) async-start(s8[9437184]{0:T(1024)(128)(4,1)} %bitcast.115), calls=%async_computation.6 | async-start | bytes 8388608
  983.9 9.3 slice-start.2
  983.9 9.3 slice-start.3
Sparse Core Ops, SparseCore 0:
  427.4 75.9 reduce-scatter.1
Sparse Core Ops, SparseCore 1:
  449.1 329.7 all-reduce.7
  785.2 190.6 all-reduce.5
